TPU v7x, 32 devices: a whole 2x2x4 slice. The times are simulated.
32 devices in a mesh: fsdp: 4 (over y, x), tenant: 4 (over z), dp: 2 (over core).
Axes of the slice: x: 2, y: 2, z: 4, core: 2. Of those that a mesh axis runs over, the one named last changes fastest.
Arguments:
- tokens: bfloat16 [3072, 5120], P(('fsdp', 'dp'), 'tenant'), may hold values from -6 to 6
- block_tenant_index: int32 [48], P(('fsdp', 'dp')), may hold values from 0 to 7
- ranks: int32 [8], replicated, may hold values from 16 to 64, as said below
- frozen_up_weight: bfloat16 [5120, 14336], P(('fsdp', 'dp'), 'tenant'), may hold values from -0.078125 to 0.078125
- tenant_down_adapters: bfloat16 [8, 64, 5120], P('tenant'), may hold values from -0.078125 to 0.078125
- tenant_up_adapters: bfloat16 [8, 64, 14336], P('tenant'), may hold values from -0.75 to 0.75
- cotangent: bfloat16 [3072, 14336], P(('fsdp', 'dp'), 'tenant'), may hold values from -6 to 6
Outputs:
- hidden_out: bfloat16 [3072, 14336], P(('fsdp', 'dp'), 'tenant')
- grad_tokens: bfloat16 [3072, 5120], P(('fsdp', 'dp'), 'tenant')
- grad_down: float32 [8, 64, 5120], P('dp', None, 'tenant')
- grad_up: float32 [8, 64, 14336], P('dp', None, 'tenant')
Inputs may be any that keep to these rules, and one draw needn't show every extreme that they name: `ranks`: multiples of 16; some tenant has rank 64.
All inputs are finite; a program needn't handle non-finite values.
Results may differ from a plain program's by a relative error of at most 0.0034.
Values may be sent and summed in bfloat16 or wider, within the bound.
A program may use at most 128 MiB of HBM per device.

v0:
```python
import jax
import jax.numpy as jnp
from jax import lax
from jax.sharding import PartitionSpec as P

BLOCK = 64
alpha_scale = 32.0
BF16 = jnp.bfloat16
F32 = jnp.float32


def nt(a, b):
    return lax.dot_general(a, b, (((1,), (1,)), ((), ())), preferred_element_type=F32)


def tn(a, b):
    return lax.dot_general(a, b, (((0,), (0,)), ((), ())), preferred_element_type=F32)


def fetch_adapter(adapter, tenant_n, dp_n):
    share = adapter.shape[1] // dp_n
    mine = lax.dynamic_slice_in_dim(adapter, lax.axis_index("dp") * share, share, axis=1)
    part = lax.all_to_all(mine, "tenant", split_axis=2, concat_axis=0, tiled=True)
    return lax.all_gather(part, "dp", axis=1, tiled=True)


def reduce_fsdp(x, fsdp_n):
    rows = x.shape[0]
    got = lax.all_to_all(
        x.astype(BF16).reshape(fsdp_n, rows // fsdp_n, x.shape[1]), "fsdp", 0, 0, tiled=True
    )
    total = jnp.sum(got.astype(F32), axis=0).astype(BF16)
    return lax.all_gather(total, "fsdp", axis=0, tiled=True).astype(F32)


def make_shards(mesh):
    tenant_n, fsdp_n, dp_n = (mesh.shape["tenant"], mesh.shape["fsdp"], mesh.shape["dp"])

    def shards(
        tokens,
        block_tenant_index,
        ranks,
        frozen_up_weight,
        tenant_down_adapters,
        tenant_up_adapters,
        cotangent,
    ):
        rows, local_d = tokens.shape
        local_f = cotangent.shape[1]
        tenants = ranks.shape[0]
        rank = tenant_down_adapters.shape[1]
        depth = frozen_up_weight.shape[0]
        blocks = fsdp_n * dp_n
        first = max(128, depth * 3 // 5 // 128 * 128) if depth > 128 else depth
        cuts = [(0, first)] + ([(first, depth)] if first < depth else [])
        weights = [
            lax.all_gather(frozen_up_weight[a:b], ("fsdp", "dp"), axis=0, tiled=True)
            for a, b in cuts
        ]
        up = fetch_adapter(tenant_up_adapters, tenant_n, dp_n).reshape(tenants * rank, local_f)
        down = fetch_adapter(tenant_down_adapters, tenant_n, dp_n).reshape(tenants * rank, local_d)
        onehot = block_tenant_index[:, None] == jnp.arange(tenants, dtype=jnp.int32)[None, :]
        sel = onehot.astype(F32)[:, None, :, None]
        own_rank = jnp.sum(jnp.where(onehot, ranks[None, :], 0), axis=1)
        keep = jnp.arange(rank, dtype=jnp.int32)[None, :] < own_rank[:, None]
        gain = jnp.where(keep, (alpha_scale / own_rank.astype(F32))[:, None], F32(0.0))

        def compact(full):
            full = full.reshape(rows // BLOCK, BLOCK, tenants, rank)
            return jnp.sum(full * sel, axis=2)

        both = jnp.concatenate([compact(nt(tokens, down)), compact(nt(cotangent, up))], axis=2)
        both = lax.psum(both, "tenant")

        def spread(values):
            scaled = (values * gain[:, None, :]).astype(BF16)
            return (scaled[:, :, None, :] * sel.astype(BF16)).reshape(rows, tenants * rank)

        adapted = spread(both[:, :, :rank])
        adapted_grad = spread(both[:, :, rank:])
        terms = jnp.concatenate([tn(adapted, cotangent), tn(adapted_grad, tokens)], axis=1)
        terms = lax.psum_scatter(terms, "dp", scatter_dimension=0, tiled=True)
        grads = reduce_fsdp(terms, fsdp_n)
        grad_up = grads[:, :local_f].reshape(tenants // dp_n, rank, local_f)
        grad_down = grads[:, local_f:].reshape(tenants // dp_n, rank, local_d)
        whole = lax.all_gather(tokens, "tenant", axis=1, tiled=True)
        whole3 = whole.reshape(rows, blocks, depth)
        hidden = jnp.dot(adapted, up, preferred_element_type=F32)
        pieces = []
        for (a, b), weight in zip(cuts, weights):
            back = nt(cotangent, weight).astype(BF16)
            n = b - a
            got = lax.all_to_all(
                back.reshape(rows, tenant_n, blocks * n // tenant_n).transpose(1, 0, 2),
                "tenant",
                0,
                0,
                tiled=True,
            )
            pieces.append(jnp.sum(got.astype(F32), axis=0).reshape(rows, blocks // tenant_n, n))
            hidden = hidden + jnp.dot(
                whole3[:, :, a:b].reshape(rows, blocks * n), weight, preferred_element_type=F32
            )
        hidden_out = hidden.astype(BF16)
        grad_base = jnp.concatenate(pieces, axis=2).reshape(rows, local_d)
        grad_tokens = (grad_base + jnp.dot(adapted_grad, down, preferred_element_type=F32)).astype(
            BF16
        )
        return (hidden_out, grad_tokens, grad_down, grad_up)

    return shards


def solution(mesh):
    return jax.shard_map(
        make_shards(mesh),
        mesh=mesh,
        in_specs=(
            P(("fsdp", "dp"), "tenant"),
            P(("fsdp", "dp")),
            P(),
            P(("fsdp", "dp"), "tenant"),
            P("tenant", None, None),
            P("tenant", None, None),
            P(("fsdp", "dp"), "tenant"),
        ),
        out_specs=(
            P(("fsdp", "dp"), "tenant"),
            P(("fsdp", "dp"), "tenant"),
            P("dp", None, "tenant"),
            P("dp", None, "tenant"),
        ),
        check_vma=False,
    )
```

profile of v0, /device:TPU:0, one launch (start us, length us, event | category | flops | bytes accessed | tf_op | source)
XLA Modules:
  0.0 595.5 jit_solution(8852192433115120866)
XLA Ops:
  7.2 1.3 constant_dynamic-slice_fusion.1
  8.5 4.0 copy.30
  12.5 4.9 reshape.171
  17.4 6.3 %all-to-all-start = ((bf16[4,2,40960]{2,1,0:T(2,128)(2,1)}), bf16[4,2,40960]{2,1,0:T(2,128)(2,1)S(1)}, u32[]{:S(2)}, u32[]{:S(2)}) async-start(bf16[4,2,40960]{2,1,0:T(2,128)(2,1)} %reshape.171), calls=%async_computation | async-start | bytes 1310720 | tf_op jit(solution)/shard_map/all_to_all | solution.py:23
  23.8 2.8 constant_dynamic-slice_fusion
  26.6 15.2 %copy.31 = bf16[2,32,14336]{1,0,2:T(2,128)(2,1)} copy(bf16[2,32,14336]{2,1,0:T(8,128)(2,1)} %constant_dynamic-slice_fusion) | data formatting | bytes 3670016
  41.9 9.4 %reshape.173 = bf16[4,2,114688]{2,1,0:T(2,128)(2,1)} reshape(bf16[14336,2,32]{2,1,0:T(2,128)(2,1)} %bitcast.65) | data formatting | bytes 3670016
  51.3 5.1 all-to-all-start.1
  56.4 2.6 reshape.172
  59.0 6.2 %copy.28 = bf16[2,32,4,1280]{3,2,1,0:T(4,128)(2,1)S(1)} copy(bf16[2,32,4,1280]{1,0,3,2:T(2,128)(2,1)} %bitcast.70) | data formatting | bytes 1310720 | tf_op jit(solution)/shard_map/all_to_all | solution.py:23
  65.2 0.9 copy.20
  66.2 32.3 %all-to-all-done.1 = bf16[4,2,114688]{2,1,0:T(2,128)(2,1)} async-done(((bf16[4,2,114688]{2,1,0:T(2,128)(2,1)}), bf16[4,2,114688]{2,1,0:T(2,128)(2,1)}, u32[]{:S(2)}, u32[]{:S(2)}) %all-to-all-start.1) | async-done | bytes 1835040 | tf_op jit(solution)/shard_map/all_to_all | solution.py:23
  98.5 6.9 %reshape.174 = bf16[14336,2,32]{2,1,0:T(2,128)(2,1)} reshape(bf16[4,2,114688]{2,1,0:T(2,128)(2,1)} %all-to-all-done.1) | data formatting | bytes 3670016
  105.4 18.1 %copy.29 = bf16[2,32,4,3584]{3,2,1,0:T(4,128)(2,1)} copy(bf16[2,32,4,3584]{1,0,3,2:T(2,128)(2,1)} %bitcast.66) | data formatting | bytes 3670016 | tf_op jit(solution)/shard_map/all_to_all | solution.py:23
  123.5 3.0 copy.24
  126.7 3.3 convolution_bitcast_fusion.1
  130.1 1.4 copy.21
  131.5 1.5 reshape.157
  132.9 5.8 all-gather.9.cloned.1.call-done
  138.7 5.0 convolution_bitcast_fusion
  143.7 1.4 copy.25
  145.1 1.5 reshape.159
  146.6 2.9 multiply_reduce_fusion.1
  149.5 0.8 pad_maximum_fusion.2
  151.4 35.2 %all-reduce.2.cloned.1.call-done = f32[6,64,128]{2,1,0:T(8,128)} async-done(((f32[6,64,128]{2,1,0:T(8,128)}), f32[6,64,128]{2,1,0:T(8,128)}) %all-reduce.2.cloned.1.call-update) | async-done | bytes 196624 | tf_op jit(solution)/shard_map/psum | solution.py:73
  186.7 1.1 fusion.3
  187.8 1.4 broadcast_multiply_fusion
  189.2 1.7 mul.91
  190.9 1.8 mul.87
  192.7 3.6 fusion.11
  196.3 5.0 fusion.10
  201.3 8.3 %pad_maximum_fusion = f32[512,4864]{1,0:T(8,128)} fusion(f32[512,1280]{1,0:T(8,128)} %fusion.11, f32[512,3584]{1,0:T(8,128)} %fusion.10), kind=kLoop, calls=%fused_computation | loop fusion | flops 2490368 | bytes 19922944 | tf_op jit(solution)/shard_map/concatenate | solution.py:81
  209.7 2.9 slice.28
  212.6 3.5 slice.26
  216.2 48.0 %all-gather.11.cloned.1.call-done = bf16[384,5120]{1,0:T(8,128)(2,1)} async-done(((bf16[384,1280]{1,0:T(8,128)(2,1)}), bf16[384,5120]{1,0:T(8,128)(2,1)}) %all-gather.11.cloned.1.call-update) | async-done | bytes 3932176 | tf_op jit(solution)/shard_map/all_gather | solution.py:86
  264.2 2.9 copy.34
  267.5 1.9 copy.35
  269.5 1.7 copy.36
  271.1 11.4 %reduce-scatter.2.cloned.1.call-done = f32[256,4864]{1,0:T(8,128)} async-done(((f32[512,4864]{1,0:T(8,128)}), f32[256,4864]{1,0:T(8,128)}) %reduce-scatter.2.cloned.1.call-update) | async-done | bytes 4980752 | tf_op jit(solution)/shard_map/reduce_scatter | solution.py:82
  282.5 4.1 convert_element_type.69
  286.6 4.6 all-to-all-start.4
  291.2 6.6 %fusion.8 = f32[384,3584]{1,0:T(8,128)} fusion(bf16[384,512]{1,0:T(8,128)(2,1)S(1)} %mul.87, bf16[512,3584]{1,0:T(8,128)(2,1)} %bitcast.82), kind=kOutput, calls=%fused_computation.33 | convolution fusion | flops 1409286144 | bytes 9568256 | tf_op jit(solution)/shard_map/dot_general | solution.py:88
  297.8 92.3 %all-gather.15.cloned.1.call-done = bf16[2048,3584]{1,0:T(8,128)(2,1)} async-done(((bf16[256,3584]{1,0:T(8,128)(2,1)}), bf16[2048,3584]{1,0:T(8,128)(2,1)}) %all-gather.15.cloned.1.call-update) | async-done | bytes 14680080 | tf_op jit(solution)/shard_map/all_gather | solution.py:57
  390.1 9.4 %convolution_convert_fusion.1 = bf16[384,2048]{1,0:T(8,128)(2,1)S(1)} fusion(bf16[384,3584]{1,0:T(8,128)(2,1)S(1)} %copy-done, bf16[2048,3584]{1,0:T(8,128)(2,1)} %all-gather.15.cloned.1.call-done), kind=kOutput, calls=%fused_computation.9 | convolution fusion | flops 5637931008 | bytes 19005440 | tf_op jit(solution)/shard_map/dot_general | solution.py:13
  399.6 1.3 copy.41
  400.9 4.6 all-to-all-start.3
  405.5 3.1 reduce_sum.62
  408.6 95.9 %all-gather.13.cloned.1.call-done = bf16[3072,3584]{1,0:T(8,128)(2,1)} async-done(((bf16[384,3584]{1,0:T(8,128)(2,1)}), bf16[3072,3584]{1,0:T(8,128)(2,1)}) %all-gather.13.cloned.1.call-update) | async-done | bytes 22020112 | tf_op jit(solution)/shard_map/all_gather | solution.py:57
  504.5 14.0 %convolution_convert_fusion = bf16[384,3072]{1,0:T(8,128)(2,1)} fusion(bf16[384,3584]{1,0:T(8,128)(2,1)S(1)} %copy-done, bf16[3072,3584]{1,0:T(8,128)(2,1)} %all-gather.13.cloned.1.call-done), kind=kOutput, calls=%fused_computation.5 | convolution fusion | flops 8456896512 | bytes 27131904 | tf_op jit(solution)/shard_map/dot_general | solution.py:13
  518.6 3.2 copy.40
  521.8 4.7 all-to-all-start.2
  526.5 11.6 %fusion.9 = f32[384,3584]{1,0:T(8,128)} fusion(bf16[384,2048]{1,0:T(8,128)(2,1)S(1)} %bitcast.87, bf16[2048,3584]{1,0:T(8,128)(2,1)} %all-gather.15.cloned.1.call-done), kind=kOutput, calls=%fused_computation.34 | convolution fusion | flops 5637144576 | bytes 21757952 | tf_op jit(solution)/shard_map/dot_general | solution.py:101
  538.1 1.7 convert_reduce_fusion.1
  539.8 1.4 reshape.166
  541.2 4.2 all-gather.17.cloned.1.call-done
  545.4 2.4 slice.36
  547.8 2.3 slice.37
  550.1 18.7 %fusion.1 = bf16[384,3584]{1,0:T(8,128)(2,1)} fusion(f32[384,3584]{1,0:T(8,128)} %fusion.9, f32[384,3584]{1,0:T(8,128)} %fusion.8, bf16[384,3072]{1,0:T(8,128)(2,1)S(1)} %bitcast.85, bf16[3072,3584]{1,0:T(8,128)(2,1)} %all-gather.13.cloned.1.call-done), kind=kOutput, calls=%fused_computation.3 | convolution fusion | flops 8459845632 | bytes 38141952 | tf_op jit(solution)/shard_map/dot_general | solution.py:101
  568.8 12.2 %all-to-all-done.2 = bf16[4,384,768]{2,1,0:T(8,128)(2,1)} async-done(((bf16[4,384,768]{2,1,0:T(8,128)(2,1)}), bf16[4,384,768]{2,1,0:T(8,128)(2,1)}, u32[]{:S(2)}, u32[]{:S(2)}) %all-to-all-start.2) | async-done | bytes 2359328 | tf_op jit(solution)/shard_map/all_to_all | solution.py:93
  581.0 2.1 convert_reduce_fusion
  583.1 0.6 reshape.164
  583.8 2.0 pad_maximum_fusion.1
  585.9 1.2 copy-done.5
  587.1 1.6 fusion.2
  (42 shorter events, 2.1 us)
Async XLA Ops:
  7.2 131.6 %copy-start = (bf16[384,3584]{1,0:T(8,128)(2,1)S(1)}, bf16[384,3584]{1,0:T(8,128)(2,1)}, u32[]{:S(2)}) copy-start(bf16[384,3584]{1,0:T(8,128)(2,1)} %param.13) | copy-start | bytes 8257540
  17.4 33.8 %all-to-all-start = ((bf16[4,2,40960]{2,1,0:T(2,128)(2,1)}), bf16[4,2,40960]{2,1,0:T(2,128)(2,1)S(1)}, u32[]{:S(2)}, u32[]{:S(2)}) async-start(bf16[4,2,40960]{2,1,0:T(2,128)(2,1)} %reshape.171), calls=%async_computation | async-start | bytes 1310720 | tf_op jit(solution)/shard_map/all_to_all | solution.py:23
  51.3 47.2 %all-to-all-start.1 = ((bf16[4,2,114688]{2,1,0:T(2,128)(2,1)}), bf16[4,2,114688]{2,1,0:T(2,128)(2,1)}, u32[]{:S(2)}, u32[]{:S(2)}) async-start(bf16[4,2,114688]{2,1,0:T(2,128)(2,1)} %reshape.173), calls=%async_computation.1 | async-start | bytes 3670016 | tf_op jit(solution)/shard_map/all_to_all | solution.py:23
  56.4 70.4 %all-gather.7.cloned.1.call-start = ((), (), s32[]{:S(2)}) async-start(), calls=%async_computation.6 | async-start | bytes 1966080 | tf_op jit(solution)/shard_map/all_gather | solution.py:24
  66.1 72.6 %all-gather.9.cloned.1.call-start = ((), (), s32[]{:S(2)}) async-start(), calls=%async_computation.7 | async-start | bytes 5505024 | tf_op jit(solution)/shard_map/all_gather | solution.py:24
  123.5 3.1 copy-start.6
  126.6 60.1 %all-reduce.2.cloned.1.call-start = ((), (), s32[]{:S(2)}) async-start(), calls=%async_computation.8 | async-start | bytes 393216 | tf_op jit(solution)/shard_map/psum | solution.py:73
  146.6 4.6 copy-start.7
  150.3 113.9 %all-gather.11.cloned.1.call-start = ((), (), s32[]{:S(2)}) async-start(), calls=%async_computation.9 | async-start | bytes 4915200 | tf_op jit(solution)/shard_map/all_gather | solution.py:86
  150.9 131.6 %reduce-scatter.2.cloned.1.call-start = ((), (), s32[]{:S(2)}) async-start(), calls=%async_computation.12 | async-start | bytes 14942208 | tf_op jit(solution)/shard_map/reduce_scatter | solution.py:82
  209.6 180.5 %all-gather.15.cloned.1.call-start = ((), (), s32[]{:S(2)}) async-start(), calls=%async_computation.11 | async-start | bytes 16515072 | tf_op jit(solution)/shard_map/all_gather | solution.py:57
  212.6 291.9 %all-gather.13.cloned.1.call-start = ((), (), s32[]{:S(2)}) async-start(), calls=%async_computation.10 | async-start | bytes 24772608 | tf_op jit(solution)/shard_map/all_gather | solution.py:57
  286.6 114.2 %all-to-all-start.4 = ((bf16[4,64,4864]{2,1,0:T(8,128)(2,1)}), bf16[4,64,4864]{2,1,0:T(8,128)(2,1)}, u32[]{:S(2)}, u32[]{:S(2)}) async-start(bf16[4,64,4864]{2,1,0:T(8,128)(2,1)} %bitcast.71), calls=%async_computation.5 | async-start | bytes 4980736 | tf_op jit(solution)/shard_map/all_to_all | solution.py:29
  400.9 120.9 %all-to-all-start.3 = ((bf16[4,384,512]{2,1,0:T(8,128)(2,1)}), bf16[4,384,512]{2,1,0:T(8,128)(2,1)}, u32[]{:S(2)}, u32[]{:S(2)}) async-start(bf16[4,384,512]{2,1,0:T(8,128)(2,1)} %bitcast.77), calls=%async_computation.3 | async-start | bytes 3145728 | tf_op jit(solution)/shard_map/all_to_all | solution.py:93
  405.5 139.9 %all-gather.17.cloned.1.call-start = ((), (), s32[]{:S(2)}) async-start(), calls=%async_computation.13 | async-start | bytes 3112960 | tf_op jit(solution)/shard_map/all_gather | solution.py:33
  521.8 4.7 copy-start.4
  521.8 59.2 %all-to-all-start.2 = ((bf16[4,384,768]{2,1,0:T(8,128)(2,1)}), bf16[4,384,768]{2,1,0:T(8,128)(2,1)}, u32[]{:S(2)}, u32[]{:S(2)}) async-start(bf16[4,384,768]{2,1,0:T(8,128)(2,1)} %bitcast.62), calls=%async_computation.2 | async-start | bytes 4718592 | tf_op jit(solution)/shard_map/all_to_all | solution.py:93
  545.4 2.4 copy-start.2
  547.8 2.3 copy-start.3
  585.8 1.3 copy-start.5
  585.8 2.9 copy-start.1
Sparse Core Ops, SparseCore 0:
  66.2 10.8 all-gather.6
  126.7 11.9 all-gather.8
  150.5 36.1 all-reduce.1
  188.1 76.0 all-gather.10
  266.4 16.1 reduce-scatter.1
  284.3 105.8 all-gather.14
  392.6 111.8 all-gather.12
  506.9 38.4 all-gather.16
where the time goes:
time: 598 us; the launch traced here: 596 us
  waiting for transfers between devices  338 us (57%)
  local copies, waits for them, and re-layouts  111 us (19%)
  matrix products  79 us (13%)
  other arithmetic  27.8 us (5%)
  starting transfers between devices  25.8 us (4%)
  between operations  14.3 us (2%)
    all_gather x2, waiting for transfers between devices, shards(): lax.all_gather(frozen_up_weight[a:b], ('fsdp', 'dp'), axis=0, tiled=True)  188 us
    unnamed x26, local copies, waits for them, and re-layouts  51 us
    all_gather x1, waiting for transfers between devices, shards(): whole = lax.all_gather(tokens, 'tenant', axis=1, tiled=True)  48 us
    psum x1, waiting for transfers between devices, shards(): both = lax.psum(both, 'tenant')  35.2 us
    all_to_all x2, waiting for transfers between devices, fetch_adapter(): lax.all_to_all(mine, 'tenant', split_axis=2, concat_axis=0, tiled=True)  32.3 us
    dot_general x4, matrix products, nt(): lax.dot_general(a, b, (((1,), (1,)), ((), ())), preferred_element_type=F32)  31.8 us
    dot_general x2, matrix products, shards(): jnp.dot(whole3[:, :, a:b].reshape(rows, blocks * n), weight, preferred_el...  30.3 us
    all_to_all x4, local copies, waits for them, and re-layouts, fetch_adapter(): lax.all_to_all(mine, 'tenant', split_axis=2, concat_axis=0, tiled=True)  28.3 us
  transfers between devices with their start and end apart: 13, of which 9 were waited for; matrix products, arithmetic and copies ran while one was open for 32% of the time, Pallas kernels for 0%

commit v1 on v0

--- a/solution.py
+++ b/solution.py
@@ -83,7 +83,7 @@
         grads = reduce_fsdp(terms, fsdp_n)
         grad_up = grads[:, :local_f].reshape(tenants // dp_n, rank, local_f)
         grad_down = grads[:, local_f:].reshape(tenants // dp_n, rank, local_d)
-        whole = lax.all_gather(tokens, "tenant", axis=1, tiled=True)
+        whole = jnp.concatenate(lax.all_gather(tokens, "tenant"), axis=1)
         whole3 = whole.reshape(rows, blocks, depth)
         hidden = jnp.dot(adapted, up, preferred_element_type=F32)
         pieces = []

time: 598 us -> 596 us (level)
  matrix products: 79 us -> 71.2 us
    all_gather x2, waiting for transfers between devices: 188 us -> 164 us  [shards(): lax.all_gather(frozen_up_weight[a:b], ('fsdp', 'dp'), axis=0, tiled=True)]
    all_gather x1, waiting for transfers between devices: 48 us -> 70.5 us  [shards(): whole = jnp.concatenate(lax.all_gather(tokens, 'tenant'), axis=1)]
    unnamed x26 -> x29, local copies, waits for them, and re-layouts: 51 us -> 44.4 us
    reshape x0 -> x1, local copies, waits for them, and re-layouts: none -> 6.26 us  [shards(): whole = jnp.concatenate(lax.all_gather(tokens, 'tenant'), axis=1)]
    slice x2, local copies, waits for them, and re-layouts: 0.34 us -> 6.47 us  [shards(): whole3[:, :, a:b].reshape(rows, blocks * n)]
  transfers between devices with their start and end apart: 13 -> 13, of which waited for: 9 -> 9; matrix products, arithmetic and copies ran while one was open for 32% -> 27% of each run, Pallas kernels for 0% -> 0%
where the time goes in v1:
time: 596 us; the launch traced here: 593 us
  waiting for transfers between devices  337 us (57%)
  local copies, waits for them, and re-layouts  116 us (19%)
  matrix products  71.2 us (12%)
  other arithmetic  27.8 us (5%)
  starting transfers between devices  25.8 us (4%)
  between operations  14.3 us (2%)
    all_gather x2, waiting for transfers between devices, shards(): lax.all_gather(frozen_up_weight[a:b], ('fsdp', 'dp'), axis=0, tiled=True)  164 us
    all_gather x1, waiting for transfers between devices, shards(): whole = jnp.concatenate(lax.all_gather(tokens, 'tenant'), axis=1)  70.5 us
    unnamed x29, local copies, waits for them, and re-layouts  44.4 us
    psum x1, waiting for transfers between devices, shards(): both = lax.psum(both, 'tenant')  36.1 us
    all_to_all x2, waiting for transfers between devices, fetch_adapter(): lax.all_to_all(mine, 'tenant', split_axis=2, concat_axis=0, tiled=True)  32.3 us
    dot_general x4, matrix products, nt(): lax.dot_general(a, b, (((1,), (1,)), ((), ())), preferred_element_type=F32)  31.8 us
    all_to_all x4, local copies, waits for them, and re-layouts, fetch_adapter(): lax.all_to_all(mine, 'tenant', split_axis=2, concat_axis=0, tiled=True)  28.3 us
    dot_general x2, matrix products, shards(): jnp.dot(whole3[:, :, a:b].reshape(rows, blocks * n), weight, preferred_el...  25.9 us
  transfers between devices with their start and end apart: 13, of which 9 were waited for; matrix products, arithmetic and copies ran while one was open for 27% of the time, Pallas kernels for 0%

profile of v1, /device:TPU:0, one launch (start us, length us, event | category | flops | bytes accessed | tf_op | source)
XLA Modules:
  0.0 592.7 jit_solution(8914918592966045438)
XLA Ops:
  7.2 1.3 constant_dynamic-slice_fusion.1
  8.5 4.0 copy.32
  12.5 4.9 reshape.172
  17.4 6.3 %all-to-all-start = ((bf16[4,2,40960]{2,1,0:T(2,128)(2,1)}), bf16[4,2,40960]{2,1,0:T(2,128)(2,1)S(1)}, u32[]{:S(2)}, u32[]{:S(2)}) async-start(bf16[4,2,40960]{2,1,0:T(2,128)(2,1)} %reshape.172), calls=%async_computation | async-start | bytes 1310720 | tf_op jit(solution)/shard_map/all_to_all | solution.py:23
  23.8 2.8 constant_dynamic-slice_fusion
  26.6 15.2 %copy.33 = bf16[2,32,14336]{1,0,2:T(2,128)(2,1)} copy(bf16[2,32,14336]{2,1,0:T(8,128)(2,1)} %constant_dynamic-slice_fusion) | data formatting | bytes 3670016
  41.9 9.4 %reshape.174 = bf16[4,2,114688]{2,1,0:T(2,128)(2,1)} reshape(bf16[14336,2,32]{2,1,0:T(2,128)(2,1)} %bitcast.67) | data formatting | bytes 3670016
  51.3 5.1 all-to-all-start.1
  56.4 2.6 reshape.173
  59.0 6.2 %copy.30 = bf16[2,32,4,1280]{3,2,1,0:T(4,128)(2,1)S(1)} copy(bf16[2,32,4,1280]{1,0,3,2:T(2,128)(2,1)} %bitcast.72) | data formatting | bytes 1310720 | tf_op jit(solution)/shard_map/all_to_all | solution.py:23
  65.2 0.9 copy.21
  66.2 32.3 %all-to-all-done.1 = bf16[4,2,114688]{2,1,0:T(2,128)(2,1)} async-done(((bf16[4,2,114688]{2,1,0:T(2,128)(2,1)}), bf16[4,2,114688]{2,1,0:T(2,128)(2,1)}, u32[]{:S(2)}, u32[]{:S(2)}) %all-to-all-start.1) | async-done | bytes 1835040 | tf_op jit(solution)/shard_map/all_to_all | solution.py:23
  98.5 6.8 %reshape.175 = bf16[14336,2,32]{2,1,0:T(2,128)(2,1)} reshape(bf16[4,2,114688]{2,1,0:T(2,128)(2,1)} %all-to-all-done.1) | data formatting | bytes 3670016
  105.3 18.1 %copy.31 = bf16[2,32,4,3584]{3,2,1,0:T(4,128)(2,1)} copy(bf16[2,32,4,3584]{1,0,3,2:T(2,128)(2,1)} %bitcast.68) | data formatting | bytes 3670016 | tf_op jit(solution)/shard_map/all_to_all | solution.py:23
  123.5 3.1 copy.25
  126.9 3.3 convolution_bitcast_fusion.1
  130.2 1.4 copy.22
  131.6 1.5 reshape.157
  133.1 5.6 all-gather.10.cloned.1.call-done
  138.7 5.0 convolution_bitcast_fusion
  143.7 1.4 copy.26
  145.1 1.5 reshape.159
  146.6 2.9 multiply_reduce_fusion.1
  149.5 0.8 pad_maximum_fusion.2
  150.6 36.1 %all-reduce.2.cloned.1.call-done = f32[6,64,128]{2,1,0:T(8,128)} async-done(((f32[6,64,128]{2,1,0:T(8,128)}), f32[6,64,128]{2,1,0:T(8,128)}) %all-reduce.2.cloned.1.call-update) | async-done | bytes 196624 | tf_op jit(solution)/shard_map/psum | solution.py:73
  186.7 1.1 fusion.3
  187.8 1.4 broadcast_multiply_fusion
  189.2 1.7 mul.91
  190.9 1.8 mul.87
  192.7 3.6 fusion.11
  196.2 5.0 fusion.10
  201.3 8.3 %pad_maximum_fusion = f32[512,4864]{1,0:T(8,128)} fusion(f32[512,1280]{1,0:T(8,128)} %fusion.11, f32[512,3584]{1,0:T(8,128)} %fusion.10), kind=kLoop, calls=%fused_computation | loop fusion | flops 2490368 | bytes 19922944 | tf_op jit(solution)/shard_map/concatenate | solution.py:81
  210.2 2.9 slice.28
  213.2 3.5 slice.26
  216.7 10.3 %reduce-scatter.2.cloned.1.call-done = f32[256,4864]{1,0:T(8,128)} async-done(((f32[512,4864]{1,0:T(8,128)}), f32[256,4864]{1,0:T(8,128)}) %reduce-scatter.2.cloned.1.call-update) | async-done | bytes 4980752 | tf_op jit(solution)/shard_map/reduce_scatter | solution.py:82
  227.0 4.1 convert_element_type.69
  231.1 4.5 all-to-all-start.4
  235.7 70.5 %all-gather.18.cloned.1.call-done = bf16[1536,1280]{1,0:T(8,128)(2,1)} async-done(((bf16[384,1280]{1,0:T(8,128)(2,1)}), bf16[1536,1280]{1,0:T(8,128)(2,1)}) %all-gather.18.cloned.1.call-update) | async-done | bytes 3932176 | tf_op jit(solution)/shard_map/all_gather | solution.py:86
  306.1 6.3 %copy.27 = bf16[384,4,1280]{0,2,1:T(8,128)(2,1)} copy(bf16[384,4,1280]{2,0,1:T(8,128)(2,1)} %bitcast.80) | data formatting | bytes 7864320 | tf_op jit(solution)/shard_map/reshape | solution.py:86
  312.4 2.9 slice.34
  315.4 3.5 slice.33
  318.9 68.4 %all-gather.14.cloned.1.call-done = bf16[2048,3584]{1,0:T(8,128)(2,1)} async-done(((bf16[256,3584]{1,0:T(8,128)(2,1)}), bf16[2048,3584]{1,0:T(8,128)(2,1)}) %all-gather.14.cloned.1.call-update) | async-done | bytes 14680080 | tf_op jit(solution)/shard_map/all_gather | solution.py:57
  387.3 9.4 %convolution_convert_fusion.1 = bf16[384,2048]{1,0:T(8,128)(2,1)S(1)} fusion(bf16[384,3584]{1,0:T(8,128)(2,1)S(1)} %copy-done, bf16[2048,3584]{1,0:T(8,128)(2,1)} %all-gather.14.cloned.1.call-done), kind=kOutput, calls=%fused_computation.9 | convolution fusion | flops 5637931008 | bytes 19005440 | tf_op jit(solution)/shard_map/dot_general | solution.py:13
  396.7 1.3 copy.40
  398.1 4.6 all-to-all-start.3
  402.7 3.1 reduce_sum.62
  405.8 95.9 %all-gather.12.cloned.1.call-done = bf16[3072,3584]{1,0:T(8,128)(2,1)} async-done(((bf16[384,3584]{1,0:T(8,128)(2,1)}), bf16[3072,3584]{1,0:T(8,128)(2,1)}) %all-gather.12.cloned.1.call-update) | async-done | bytes 22020112 | tf_op jit(solution)/shard_map/all_gather | solution.py:57
  501.7 14.1 %convolution_convert_fusion = bf16[384,3072]{1,0:T(8,128)(2,1)} fusion(bf16[384,3584]{1,0:T(8,128)(2,1)S(1)} %copy-done, bf16[3072,3584]{1,0:T(8,128)(2,1)} %all-gather.12.cloned.1.call-done), kind=kOutput, calls=%fused_computation.5 | convolution fusion | flops 8456896512 | bytes 27131904 | tf_op jit(solution)/shard_map/dot_general | solution.py:13
  515.8 3.2 copy.39
  519.0 4.8 all-to-all-start.2
  523.8 11.6 %fusion.9 = f32[384,3584]{1,0:T(8,128)} fusion(bf16[384,2048]{0,1:T(8,128)(2,1)S(1)} %bitcast.79, bf16[2048,3584]{1,0:T(8,128)(2,1)} %all-gather.14.cloned.1.call-done), kind=kOutput, calls=%fused_computation.34 | convolution fusion | flops 5637144576 | bytes 21757952 | tf_op jit(solution)/shard_map/dot_general | solution.py:101
  535.4 1.7 convert_reduce_fusion.1
  537.1 1.4 reshape.166
  538.5 4.1 all-gather.16.cloned.1.call-done
  542.6 2.4 slice.36
  545.0 2.3 slice.37
  547.3 14.3 %fusion.8 = f32[384,3584]{1,0:T(8,128)S(1)} fusion(bf16[384,3072]{0,1:T(8,128)(2,1)S(1)} %bitcast.86, bf16[3072,3584]{1,0:T(8,128)(2,1)} %all-gather.12.cloned.1.call-done), kind=kOutput, calls=%fused_computation.33 | convolution fusion | flops 8455716864 | bytes 29884416 | tf_op jit(solution)/shard_map/dot_general | solution.py:101
  561.6 3.2 fusion.1
  564.8 13.3 %all-to-all-done.2 = bf16[4,384,768]{2,1,0:T(8,128)(2,1)} async-done(((bf16[4,384,768]{2,1,0:T(8,128)(2,1)}), bf16[4,384,768]{2,1,0:T(8,128)(2,1)}, u32[]{:S(2)}, u32[]{:S(2)}) %all-to-all-start.2) | async-done | bytes 2359328 | tf_op jit(solution)/shard_map/all_to_all | solution.py:93
  578.2 2.1 convert_reduce_fusion
  580.3 0.6 reshape.164
  580.9 2.0 pad_maximum_fusion.1
  583.1 1.2 copy-done.6
  584.2 1.6 fusion.2
  (47 shorter events, 1.6 us)
Async XLA Ops:
  7.2 131.5 %copy-start = (bf16[384,3584]{1,0:T(8,128)(2,1)S(1)}, bf16[384,3584]{1,0:T(8,128)(2,1)}, u32[]{:S(2)}) copy-start(bf16[384,3584]{1,0:T(8,128)(2,1)} %param.13) | copy-start | bytes 8257540
  17.4 33.8 %all-to-all-start = ((bf16[4,2,40960]{2,1,0:T(2,128)(2,1)}), bf16[4,2,40960]{2,1,0:T(2,128)(2,1)S(1)}, u32[]{:S(2)}, u32[]{:S(2)}) async-start(bf16[4,2,40960]{2,1,0:T(2,128)(2,1)} %reshape.172), calls=%async_computation | async-start | bytes 1310720 | tf_op jit(solution)/shard_map/all_to_all | solution.py:23
  51.3 47.2 %all-to-all-start.1 = ((bf16[4,2,114688]{2,1,0:T(2,128)(2,1)}), bf16[4,2,114688]{2,1,0:T(2,128)(2,1)}, u32[]{:S(2)}, u32[]{:S(2)}) async-start(bf16[4,2,114688]{2,1,0:T(2,128)(2,1)} %reshape.174), calls=%async_computation.1 | async-start | bytes 3670016 | tf_op jit(solution)/shard_map/all_to_all | solution.py:23
  56.4 70.5 %all-gather.8.cloned.1.call-start = ((), (), s32[]{:S(2)}) async-start(), calls=%async_computation.6 | async-start | bytes 1966080 | tf_op jit(solution)/shard_map/all_gather | solution.py:24
  66.1 72.6 %all-gather.10.cloned.1.call-start = ((), (), s32[]{:S(2)}) async-start(), calls=%async_computation.7 | async-start | bytes 5505024 | tf_op jit(solution)/shard_map/all_gather | solution.py:24
  123.4 3.1 copy-start.7
  123.4 3.1 copy-start.8
  126.5 60.1 %all-reduce.2.cloned.1.call-start = ((), (), s32[]{:S(2)}) async-start(), calls=%async_computation.8 | async-start | bytes 393216 | tf_op jit(solution)/shard_map/psum | solution.py:73
  150.3 76.7 %reduce-scatter.2.cloned.1.call-start = ((), (), s32[]{:S(2)}) async-start(), calls=%async_computation.11 | async-start | bytes 14942208 | tf_op jit(solution)/shard_map/reduce_scatter | solution.py:82
  209.6 96.6 %all-gather.18.cloned.1.call-start = ((), (), s32[]{:S(2)}) async-start(), calls=%async_computation.13 | async-start | bytes 4915200 | tf_op jit(solution)/shard_map/all_gather | solution.py:86
  210.2 177.2 %all-gather.14.cloned.1.call-start = ((), (), s32[]{:S(2)}) async-start(), calls=%async_computation.10 | async-start | bytes 16515072 | tf_op jit(solution)/shard_map/all_gather | solution.py:57
  213.1 288.6 %all-gather.12.cloned.1.call-start = ((), (), s32[]{:S(2)}) async-start(), calls=%async_computation.9 | async-start | bytes 24772608 | tf_op jit(solution)/shard_map/all_gather | solution.py:57
  231.1 166.9 %all-to-all-start.4 = ((bf16[4,64,4864]{2,1,0:T(8,128)(2,1)}), bf16[4,64,4864]{2,1,0:T(8,128)(2,1)}, u32[]{:S(2)}, u32[]{:S(2)}) async-start(bf16[4,64,4864]{2,1,0:T(8,128)(2,1)} %bitcast.73), calls=%async_computation.5 | async-start | bytes 4980736 | tf_op jit(solution)/shard_map/all_to_all | solution.py:29
  398.1 120.9 %all-to-all-start.3 = ((bf16[4,384,512]{2,1,0:T(8,128)(2,1)}), bf16[4,384,512]{2,1,0:T(8,128)(2,1)}, u32[]{:S(2)}, u32[]{:S(2)}) async-start(bf16[4,384,512]{2,1,0:T(8,128)(2,1)} %bitcast.78), calls=%async_computation.3 | async-start | bytes 3145728 | tf_op jit(solution)/shard_map/all_to_all | solution.py:93
  402.7 139.9 %all-gather.16.cloned.1.call-start = ((), (), s32[]{:S(2)}) async-start(), calls=%async_computation.12 | async-start | bytes 3112960 | tf_op jit(solution)/shard_map/all_gather | solution.py:33
  518.9 4.9 copy-start.3
  519.0 59.2 %all-to-all-start.2 = ((bf16[4,384,768]{2,1,0:T(8,128)(2,1)}), bf16[4,384,768]{2,1,0:T(8,128)(2,1)}, u32[]{:S(2)}, u32[]{:S(2)}) async-start(bf16[4,384,768]{2,1,0:T(8,128)(2,1)} %bitcast.62), calls=%async_computation.2 | async-start | bytes 4718592 | tf_op jit(solution)/shard_map/all_to_all | solution.py:93
  542.6 2.4 copy-start.2
  545.0 2.3 copy-start.5
  545.0 16.6 %slice-start = ((s8[5505024]{0:T(1024)(128)(4,1)}), s8[4194304]{0:T(1024)(128)(4,1)S(1)}, s32[]{:S(2)}) async-start(s8[5505024]{0:T(1024)(128)(4,1)} %bitcast.65), calls=%async_computation.14 | async-start | bytes 8388608
  547.3 14.3 %slice-start.1 = ((s8[5505024]{0:T(1024)(128)(4,1)}), s8[1310720]{0:T(1024)(128)(4,1)S(1)}, s32[]{:S(2)}) async-start(s8[5505024]{0:T(1024)(128)(4,1)} %bitcast.65), calls=%async_computation.15 | async-start | bytes 2621440
  547.3 14.3 %copy-start.4 = (bf16[8,64,3584]{2,1,0:T(8,128)(2,1)S(1)}, bf16[8,64,3584]{2,1,0:T(8,128)(2,1)}, u32[]{:S(2)}) copy-start(bf16[8,64,3584]{2,1,0:T(8,128)(2,1)} %all-gather.10.cloned.1.call-done) | copy-start | bytes 11010052
  582.9 1.3 copy-start.6
  582.9 2.9 copy-start.1
Sparse Core Ops, SparseCore 0:
  66.2 10.8 all-gather.7
  126.7 11.9 all-gather.9
  150.4 36.1 all-reduce.1
  209.7 17.2 reduce-scatter.1
  228.4 77.6 all-gather.17
  307.9 79.3 all-gather.13
  389.8 111.8 all-gather.11
  504.1 38.4 all-gather.15
